TPU v7x, 32 devices: a whole 2x2x4 slice. The times are simulated.
32 devices in a mesh: tm: 4 (over z), batch: 4 (over x, core), width: 2 (over y).
Axes of the slice: x: 2, y: 2, z: 4, core: 2. Of those that a mesh axis runs over, the one named last changes fastest.
Arguments:
- moves: int32 [8, 1024], P('batch', 'tm'), may hold values from 0 to 361
- lengths: int32 [8], P('batch'), may hold values from 1 to 1024
- outcomes: int32 [8], P('batch'), may hold values from -1 to 1
- embedded: bfloat16 [8, 1024, 2048], P('batch', 'tm', 'width'), may hold values from -6 to 6
- w_branches: bfloat16 [4, 2048, 2048], P(None, ('tm', 'batch'), 'width'), may hold values from -0.125 to 0.125
- conv_w: float32 [4, 2048], P(None, 'width'), may hold values from -3 to 3
- gate_bias: float32 [2, 2048], P(None, 'width'), may hold values from -4 to 4
- rates: float32 [2048], P('width'), may hold values from 0.001 to 0.105
- w_down: bfloat16 [2048, 2048], P(('tm', 'batch'), 'width'), may hold values from -0.125 to 0.125
- w_policy: bfloat16 [2048, 362], P('width'), may hold values from -12 to 12
- w_value: bfloat16 [2048], P('width'), may hold values from -0.125 to 0.125
Outputs:
- position_loss: float32 [8, 1024], P('batch', 'tm')
- value: float32 [8, 1024], P('batch', 'tm')
All inputs are finite; a program needn't handle non-finite values.
Results may differ from a plain program's by a relative error of at most 0.0033.
Values may be sent and summed in bfloat16 or wider, within the bound.
A program may use at most 128 MiB of HBM per device.

v0:
```python
import jax
import jax.numpy as jnp
from jax import lax
from jax.sharding import PartitionSpec as P

D = 2048
KERNEL = 4


def from_behind(value, axis, steps):
    count = lax.axis_size(axis)
    initial, last = (max(0, -steps), min(count, count - steps))
    return lax.ppermute(value, axis, [(source, source + steps) for source in range(initial, last)])


def link(early, late):
    return (early[0] + late[0], jnp.exp(late[0]) * early[1] + late[1])


def shards(
    moves,
    lengths,
    outcomes,
    embedded,
    w_branches,
    conv_w,
    gate_bias,
    rates,
    w_down,
    w_policy,
    w_value,
):
    games, block_len, half = embedded.shape
    count = games * block_len
    chans = w_branches.shape[2]
    features = lax.all_gather(embedded, "width", axis=2, tiled=True).reshape(count, -1)
    proj = jnp.einsum(
        "td,kdn->ktn",
        features,
        lax.all_gather(w_branches, ("tm", "batch"), axis=1, tiled=True),
        preferred_element_type=jnp.float32,
    )
    proj = proj.reshape(4, games, block_len, chans)
    gated = jax.nn.gelu(proj[0])
    source = proj[1]
    prior = from_behind(source[:, block_len - (KERNEL - 1) :, :], "tm", 1)
    extended = jnp.concatenate([prior, source], 1)
    conv = jnp.zeros((games, block_len, chans), jnp.float32)
    for k in range(KERNEL):
        conv = conv + conv_w[k] * extended[:, KERNEL - 1 - k : KERNEL - 1 - k + block_len]
    recur = jax.nn.sigmoid(proj[2] + gate_bias[0])
    inflow = jax.nn.sigmoid(proj[3] + gate_bias[1])
    log_a = -8.0 * recur * rates
    decay = jnp.exp(log_a)
    drive = jnp.sqrt(1.0 - decay * decay) * inflow * conv
    summed, local = lax.associative_scan(link, (log_a, drive), axis=1)
    block_decay = jnp.exp(summed[:, -1])
    block_end = local[:, -1]

    def relay(step, state):
        outgoing, _ = state
        arrived = from_behind(outgoing, "tm", 1)
        return (block_decay * arrived + block_end, arrived)

    _, incoming = lax.fori_loop(
        0, lax.axis_size("tm") - 1, relay, (block_end, jnp.zeros_like(block_end))
    )
    hidden = local + jnp.exp(summed) * incoming[:, None, :]
    mixed = (hidden * gated).astype(jnp.bfloat16).reshape(count, chans)
    partial_down = lax.dot_general(
        mixed,
        lax.all_gather(w_down, ("tm", "batch"), axis=0, tiled=True),
        (((1,), (1,)), ((), ())),
        preferred_element_type=jnp.float32,
    )
    down = lax.psum_scatter(partial_down, "width", scatter_dimension=1, tiled=True)
    resid = (embedded.reshape(count, half).astype(jnp.float32) + down).astype(jnp.bfloat16)
    wide = resid.astype(jnp.float32)
    local_sq = jnp.sum(wide * wide, -1)
    local_logits = jnp.dot(resid, w_policy, preferred_element_type=jnp.float32)
    local_value = jnp.dot(resid, w_value, preferred_element_type=jnp.float32)
    raw_logits, raw_value, sumsq = lax.psum((local_logits, local_value, local_sq), "width")
    norm = lax.rsqrt(sumsq / D + 1e-06)
    logits = raw_logits * norm[:, None]
    value = jnp.tanh(raw_value * norm)
    top = jnp.max(logits, -1, keepdims=True)
    lse = top[:, 0] + jnp.log(jnp.sum(jnp.exp(logits - top), -1))
    column = lax.broadcasted_iota(jnp.int32, logits.shape, 1)
    picked = jnp.sum(jnp.where(column == moves.reshape(count, 1), logits, 0.0), -1)
    target = jnp.broadcast_to(outcomes.astype(jnp.float32)[:, None], (games, block_len)).reshape(
        count
    )
    position = lax.axis_index("tm") * block_len + lax.broadcasted_iota(
        jnp.int32, (games, block_len), 1
    )
    where_live = (position < lengths[:, None]).reshape(count)
    loss = jnp.where(where_live, lse - picked + (value - target) ** 2, 0.0)
    return (loss.reshape(games, block_len), value.reshape(games, block_len))


def solution(mesh):
    in_specs = (
        P("batch", "tm"),
        P("batch"),
        P("batch"),
        P("batch", "tm", "width"),
        P(None, ("tm", "batch"), "width"),
        P(None, "width"),
        P(None, "width"),
        P("width"),
        P(("tm", "batch"), "width"),
        P("width", None),
        P("width"),
    )
    out_specs = (P("batch", "tm"), P("batch", "tm"))
    return jax.shard_map(shards, mesh=mesh, in_specs=in_specs, out_specs=out_specs, check_vma=False)
```

profile of v0, /device:TPU:0, one launch (start us, length us, event | category | flops | bytes accessed | tf_op | source)
XLA Modules:
  0.0 492.6 jit_solution(15699372225943647497)
XLA Ops:
  9.5 35.9 %all-gather.6.cloned.1.call-done = bf16[2,256,2048]{2,1,0:T(8,128)(2,1)} async-done(((bf16[2,256,1024]{2,1,0:T(8,128)(2,1)}), bf16[2,256,2048]{2,1,0:T(8,128)(2,1)}) %all-gather.6.cloned.1.call-update) | async-done | bytes 2097168 | tf_op jit(solution)/shard_map/all_gather | solution.py:36
  45.4 128.7 %all-gather.4.cloned.1.call-done = bf16[4,2048,1024]{2,1,0:T(8,128)(2,1)} async-done(((bf16[4,128,1024]{2,1,0:T(8,128)(2,1)}), bf16[4,2048,1024]{2,1,0:T(8,128)(2,1)}) %all-gather.4.cloned.1.call-update) | async-done | bytes 16777232 | tf_op jit(solution)/shard_map/all_gather | solution.py:40
  174.1 12.5 %convolution_bitcast_fusion = f32[4,512,1024]{2,1,0:T(8,128)S(1)} fusion(bf16[512,2048,1]{1,0,2:T(8,128)(2,1)} %bitcast.75, bf16[4,2048,1024]{2,1,0:T(8,128)(2,1)} %all-gather.4.cloned.1.call-done), kind=kOutput, calls=%fused_computation.1 | convolution fusion | flops 8589934592 | bytes 27262976 | tf_op jit(solution)/shard_map/td,kdn->ktn/dot_general | solution.py:37
  186.6 2.9 fusion.30
  194.2 7.6 %fusion.4 = (f32[2,256,1024]{2,1,0:T(8,128)S(1)}, f32[2,256,1024]{2,1,0:T(8,128)}) fusion(f32[2,3,1024]{2,1,0:T(4,128)S(1)} %collective-permute-done.1, f32[2,256,1024]{2,1,0:T(8,128)} %bitcast.47, f32[2,256,1024]{2,1,0:T(8,128)} %bitcast.50, f32[1024]{0:T(1024)S(1)} %bitcast.69, f32[1024]{0:T(1024)S(1)} %bitcast.70, f32[1024]{0:T(1024)S(1)} %bitcast.68, ...), kind=kLoop, calls=%fused_computation.9 | loop fusion | flops 12058624 | bytes 10539008 | tf_op jit(solution)/shard_map/mul | solution.py:55
  204.6 2.9 slice.299
  207.5 5.4 %slice.297 = f32[2,128,1024]{2,1,0:T(8,128)} slice(f32[2,256,1024]{2,1,0:T(8,128)} %get-tuple-element.48), slice={[0:2:1], [1:256:2], [0:1024:1]} | slice | bytes 2097152 | tf_op jit(solution)/shard_map/slice | solution.py:56
  212.9 5.5 %slice.301 = f32[2,128,1024]{2,1,0:T(8,128)} slice(f32[2,256,1024]{2,1,0:T(8,128)} %get-tuple-element.48), slice={[0:2:1], [0:255:2], [0:1024:1]} | slice | bytes 2097152 | tf_op jit(solution)/shard_map/slice | solution.py:56
  218.4 4.2 multiply_add_fusion.1
  222.5 3.3 slice.304
  225.8 3.3 slice.305
  229.1 3.3 slice.303
  232.3 3.2 slice.307
  290.1 3.3 slice.302
  293.4 3.3 slice.351
  299.6 5.6 %slice.296 = f32[2,127,1024]{2,1,0:T(8,128)} slice(f32[2,256,1024]{2,1,0:T(8,128)} %get-tuple-element.48), slice={[0:2:1], [2:256:2], [0:1024:1]} | slice | bytes 2080768 | tf_op jit(solution)/shard_map/slice | solution.py:56
  305.2 3.0 slice.353
  318.5 5.5 %pad.129 = f32[2,256,1024]{2,1,0:T(8,128)} pad(f32[2,128,1024]{2,1,0:T(8,128)} %add.338, f32[]{:T(128)} %constant.6.clone.1), padding=0_0_0x1_0_1x0_0_0 | pad | bytes 3145732 | tf_op jit(solution)/shard_map/pad | solution.py:56
  325.8 3.0 pad.110
  333.7 2.9 fusion.19
  337.8 5.4 %pad.128 = f32[2,256,1024]{2,1,0:T(8,128)} pad(f32[2,128,1024]{2,1,0:T(8,128)} %pad_maximum_fusion.2, f32[]{:T(128)} %constant.6.clone.1), padding=0_0_0x0_1_1x0_0_0 | pad | bytes 3145732 | tf_op jit(solution)/shard_map/pad | solution.py:56
  344.1 5.5 %pad.113 = f32[2,256,1024]{2,1,0:T(8,128)} pad(f32[2,128,1024]{2,1,0:T(8,128)} %add.322, f32[]{:T(128)} %constant.6.clone.1), padding=0_0_0x1_0_1x0_0_0 | pad | bytes 3145732 | tf_op jit(solution)/shard_map/pad | solution.py:56
  351.9 5.5 %pad.112 = f32[2,256,1024]{2,1,0:T(8,128)} pad(f32[2,128,1024]{2,1,0:T(8,128)} %pad_maximum_fusion.1, f32[]{:T(128)} %constant.6.clone.1), padding=0_0_0x0_1_1x0_0_0 | pad | bytes 3145732 | tf_op jit(solution)/shard_map/pad | solution.py:56
  358.4 18.6 %while.12 = (s32[]{:T(128)}, f32[2,1024]{1,0:T(2,128)S(1)}, f32[2,1024]{1,0:T(2,128)}, f32[2,1024]{1,0:T(2,128)S(1)}, f32[2,1024]{1,0:T(2,128)S(1)}, /*index=5*/s32[]{:T(128)}) while((s32[]{:T(128)}, f32[2,1024]{1,0:T(2,128)S(1)}, f32[2,1024]{1,0:T(2,128)}, f32[2,1024]{1,0:T(2,128)S(1)}, f32[2,1024]{1,0:T(2,128)S(1)}, ...), condition=%wide.region_1.0_spmd, body=%wide.region_0.0_spmd.sunk | while | flops 4098 | bytes 98441 | solution.py:65
  358.4 4.4 collective-permute-start
  364.7 4.2 collective-permute-start
  370.8 4.2 collective-permute-start
  377.0 5.8 %fusion.16 = bf16[2,256,1024]{2,1,0:T(8,128)(2,1)} fusion(f32[2,256,1024]{2,1,0:T(8,128)} %bitcast.48, f32[2,256,1024]{2,1,0:T(8,128)} %pad.128, f32[2,256,1024]{2,1,0:T(8,128)S(1)} %copy-done.4, f32[2,256,1024]{2,1,0:T(8,128)} %pad.112, f32[2,256,1024]{2,1,0:T(8,128)} %pad.113, f32[2,1024]{1,0:T(2,128)} %get-tuple-element.28), kind=kLoop, calls=%fused_computation.21 | loop fusion | flops 7340032 | bytes 11542528 | tf_op jit(solution)/shard_map/convert_element_type | solution.py:69
  382.8 6.9 %fusion.35 = f32[512,2048]{1,0:T(8,128)} fusion(bf16[512,1024]{1,0:T(8,128)(2,1)} %bitcast.51, bf16[2048,1024]{1,0:T(8,128)(2,1)} %all-gather.8.cloned.1.call-done), kind=kOutput, calls=%fused_computation.100 | convolution fusion | flops 2147483648 | bytes 9437184 | tf_op jit(solution)/shard_map/dot_general | solution.py:70
  389.7 55.3 %reduce-scatter.2.cloned.1.call-done = f32[512,1024]{1,0:T(8,128)} async-done(((f32[512,2048]{1,0:T(8,128)}), f32[512,1024]{1,0:T(8,128)}) %reduce-scatter.2.cloned.1.call-update) | async-done | bytes 2097168 | tf_op jit(solution)/shard_map/reduce_scatter | solution.py:76
  449.1 4.9 all-reduce.32
  454.1 28.3 %all-reduce.35.cloned.1.call-done = f32[512,362]{0,1:T(8,128)} async-done(((f32[512,362]{0,1:T(8,128)}), f32[512,362]{0,1:T(8,128)}) %all-reduce.35.cloned.1.call-update) | async-done | bytes 741392 | tf_op jit(solution)/shard_map/psum | solution.py:82
  (233 shorter events, 102.8 us)
Async XLA Ops:
  7.2 439.9 %copy-start = (bf16[1024,362]{0,1:T(8,128)(2,1)S(1)}, bf16[1024,362]{0,1:T(8,128)(2,1)}, u32[]{:S(2)}) copy-start(bf16[1024,362]{0,1:T(8,128)(2,1)} %param.22) | copy-start | bytes 2224132
  7.2 2.3 copy-start.34
  7.2 38.2 %all-gather.6.cloned.1.call-start = ((), (), s32[]{:S(2)}) async-start(), calls=%async_computation.2 | async-start | bytes 3145728 | tf_op jit(solution)/shard_map/all_gather | solution.py:36
  7.9 166.1 %all-gather.4.cloned.1.call-start = ((), (), s32[]{:S(2)}) async-start(), calls=%async_computation.1 | async-start | bytes 17825792 | tf_op jit(solution)/shard_map/all_gather | solution.py:40
  8.7 374.1 %all-gather.8.cloned.1.call-start = ((), (), s32[]{:S(2)}) async-start(), calls=%async_computation.3 | async-start | bytes 4456448 | tf_op jit(solution)/shard_map/all_gather | solution.py:72
  9.4 435.6 %reduce-scatter.2.cloned.1.call-start = ((), (), s32[]{:S(2)}) async-start(), calls=%async_computation.4 | async-start | bytes 6291456 | tf_op jit(solution)/shard_map/reduce_scatter | solution.py:76
  186.6 6.1 %copy-start.35 = (f32[1024]{0:T(1024)S(1)}, f32[1024]{0:T(1024)}, u32[]{:S(2)}) copy-start(f32[1024]{0:T(1024)} %param.20) | copy-start | bytes 12292
  190.9 3.3 collective-permute-start.1
  299.6 10.6 %copy-start.18 = (f32[2,2,1024]{2,1,0:T(2,128)S(1)}, f32[2,2,1024]{2,1,0:T(2,128)}, u32[]{:S(2)}) copy-start(f32[2,2,1024]{2,1,0:T(2,128)} %slice.335) | copy-start | bytes 49156
  299.6 10.6 %copy-start.19 = (f32[2,2,1024]{2,1,0:T(2,128)S(1)}, f32[2,2,1024]{2,1,0:T(2,128)}, u32[]{:S(2)}) copy-start(f32[2,2,1024]{2,1,0:T(2,128)} %slice.333) | copy-start | bytes 49156
  299.6 10.6 %copy-start.20 = (f32[2,2,1024]{2,1,0:T(2,128)S(1)}, f32[2,2,1024]{2,1,0:T(2,128)}, u32[]{:S(2)}) copy-start(f32[2,2,1024]{2,1,0:T(2,128)} %slice.337) | copy-start | bytes 49156
  299.6 10.8 %copy-start.15 = (f32[1,8,1024]{2,1,0:T(8,128)S(1)}, f32[1,8,1024]{2,1,0:T(8,128)}, u32[]{:S(2)}) copy-start(f32[1,8,1024]{2,1,0:T(8,128)} %get-tuple-element.103) | copy-start | bytes 98308
  299.6 11.1 %copy-start.16 = (f32[2,3,1024]{2,1,0:T(4,128)S(1)}, f32[2,3,1024]{2,1,0:T(4,128)}, u32[]{:S(2)}) copy-start(f32[2,3,1024]{2,1,0:T(4,128)} %slice.326) | copy-start | bytes 73732
  299.6 11.1 %copy-start.17 = (f32[2,3,1024]{2,1,0:T(4,128)S(1)}, f32[2,3,1024]{2,1,0:T(4,128)}, u32[]{:S(2)}) copy-start(f32[2,3,1024]{2,1,0:T(4,128)} %slice.343) | copy-start | bytes 73732
  305.2 5.6 %copy-start.32 = (f32[2,1,1024]{2,1,0:T(1,128)S(1)}, f32[2,1,1024]{2,1,0:T(1,128)}, u32[]{:S(2)}) copy-start(f32[2,1,1024]{2,1,0:T(1,128)} %slice.411) | copy-start | bytes 24580
  305.2 5.7 %copy-start.31 = (f32[2,1,1024]{2,1,0:T(1,128)S(1)}, f32[2,1,1024]{2,1,0:T(1,128)}, u32[]{:S(2)}) copy-start(f32[2,1,1024]{2,1,0:T(1,128)} %slice.385) | copy-start | bytes 24580
  305.2 5.8 %copy-start.13 = (f32[2,7,1024]{2,1,0:T(8,128)S(1)}, f32[2,7,1024]{2,1,0:T(8,128)}, u32[]{:S(2)}) copy-start(f32[2,7,1024]{2,1,0:T(8,128)} %slice.320) | copy-start | bytes 172036
  305.2 5.8 %copy-start.14 = (f32[2,7,1024]{2,1,0:T(8,128)S(1)}, f32[2,7,1024]{2,1,0:T(8,128)}, u32[]{:S(2)}) copy-start(f32[2,7,1024]{2,1,0:T(8,128)} %slice.345) | copy-start | bytes 172036
  305.2 5.9 %copy-start.30 = (f32[2,1,1024]{2,1,0:T(1,128)S(1)}, f32[2,1,1024]{2,1,0:T(1,128)}, u32[]{:S(2)}) copy-start(f32[2,1,1024]{2,1,0:T(1,128)} %slice.410) | copy-start | bytes 24580
  308.2 3.1 copy-start.29
  318.5 5.5 %copy-start.23 = (f32[2,1,1024]{2,1,0:T(1,128)S(1)}, f32[2,1,1024]{2,1,0:T(1,128)}, u32[]{:S(2)}) copy-start(f32[2,1,1024]{2,1,0:T(1,128)} %slice.381) | copy-start | bytes 24580
  330.9 2.9 copy-start.1
  330.9 2.9 copy-start.2
  330.9 2.9 copy-start.6
  333.7 2.9 copy-start.22
  337.8 5.4 %copy-start.4 = (f32[2,256,1024]{2,1,0:T(8,128)S(1)}, f32[2,256,1024]{2,1,0:T(8,128)}, u32[]{:S(2)}) copy-start(f32[2,256,1024]{2,1,0:T(8,128)} %pad.129) | copy-start | bytes 6291460
  343.2 6.4 %copy-start.21 = (f32[2,1,1024]{2,1,0:T(1,128)S(1)}, f32[2,1,1024]{2,1,0:T(1,128)}, u32[]{:S(2)}) copy-start(f32[2,1,1024]{2,1,0:T(1,128)} %slice.380) | copy-start | bytes 24580
  358.4 5.7 %collective-permute-start = (f32[2,1024]{1,0:T(2,128)S(1)}, f32[2,1024]{1,0:T(2,128)S(1)}, u32[]{:S(2)}, u32[]{:S(2)}) collective-permute-start(f32[2,1024]{1,0:T(2,128)S(1)} %get-tuple-element.135), channel_id=1, source_target_pairs={{0,8},{8,16},{16,24},{1,9},{9,17},{17,25},{2,10},{10,18},{18,26},{... | collective-permute-start | bytes 24584 | tf_op jit(solution)/shard_map/while/body/eval_jaxpr/ppermute | solution.py:13
  364.7 5.5 %collective-permute-start = (f32[2,1024]{1,0:T(2,128)S(1)}, f32[2,1024]{1,0:T(2,128)S(1)}, u32[]{:S(2)}, u32[]{:S(2)}) collective-permute-start(f32[2,1024]{1,0:T(2,128)S(1)} %get-tuple-element.135), channel_id=1, source_target_pairs={{0,8},{8,16},{16,24},{1,9},{9,17},{17,25},{2,10},{10,18},{18,26},{... | collective-permute-start | bytes 24584 | tf_op jit(solution)/shard_map/while/body/eval_jaxpr/ppermute | solution.py:13
  370.8 5.5 %collective-permute-start = (f32[2,1024]{1,0:T(2,128)S(1)}, f32[2,1024]{1,0:T(2,128)S(1)}, u32[]{:S(2)}, u32[]{:S(2)}) collective-permute-start(f32[2,1024]{1,0:T(2,128)S(1)} %get-tuple-element.135), channel_id=1, source_target_pairs={{0,8},{8,16},{16,24},{1,9},{9,17},{17,25},{2,10},{10,18},{18,26},{... | collective-permute-start | bytes 24584 | tf_op jit(solution)/shard_map/while/body/eval_jaxpr/ppermute | solution.py:13
  389.6 55.4 %copy-start.5 = (bf16[2,256,1024]{2,1,0:T(8,128)(2,1)S(1)}, bf16[2,256,1024]{2,1,0:T(8,128)(2,1)}, u32[]{:S(2)}) copy-start(bf16[2,256,1024]{2,1,0:T(8,128)(2,1)} %param.16) | copy-start | bytes 3145732
  389.7 92.7 %all-reduce.35.cloned.1.call-start = ((), (), s32[]{:S(2)}) async-start(), calls=%async_computation.5 | async-start | bytes 1507328 | tf_op jit(solution)/shard_map/psum | solution.py:82
  (19 other events, 21.4 us)
Sparse Core Ops, SparseCore 0:
  9.6 35.8 all-gather.5
  47.6 126.4 all-gather.3
  176.2 48.9 all-gather.7
  389.8 55.1 reduce-scatter.1
  448.7 33.6 all-reduce.34
where the time goes:
time: 496 us; the launch traced here: 493 us
  waiting for transfers between devices  256 us (52%)
  local copies, waits for them, and re-layouts  133 us (27%)
  other arithmetic  48.4 us (10%)
  matrix products  21.2 us (4%)
  starting transfers between devices  14.7 us (3%)
  between operations  14.6 us (3%)
    all_gather x1, waiting for transfers between devices, shards(): lax.all_gather(w_branches, ('tm', 'batch'), axis=1, tiled=True)  129 us
    slice x52, local copies, waits for them, and re-layouts, shards(): summed, local = lax.associative_scan(link, (log_a, drive), axis=1)  94.9 us
    reduce_scatter x1, waiting for transfers between devices, shards(): lax.psum_scatter(partial_down, 'width', scatter_dimension=1, tiled=True)  55.3 us
    all_gather x1, waiting for transfers between devices, shards(): lax.all_gather(embedded, 'width', axis=2, tiled=True).reshape(count, -1)  35.9 us
    pad x28, local copies, waits for them, and re-layouts, shards(): summed, local = lax.associative_scan(link, (log_a, drive), axis=1)  29.4 us
    psum x1, waiting for transfers between devices, shards(): lax.psum((local_logits, local_value, local_sq), 'width')  28.3 us
    add x13, other arithmetic, link(): return (early[0] + late[0], jnp.exp(late[0]) * early[1] + late[1])  17.8 us
    ppermute x4, starting transfers between devices, from_behind(): lax.ppermute(value, axis, [(source, source + steps) for source in range(i...  14.6 us
  transfers between devices with their start and end apart: 9, of which 8 were waited for; matrix products, arithmetic and copies ran while one was open for 37% of the time, Pallas kernels for 0%

commit v1 on v0

--- a/solution.py
+++ b/solution.py
@@ -37,7 +37,7 @@
     proj = jnp.einsum(
         "td,kdn->ktn",
         features,
-        lax.all_gather(w_branches, ("tm", "batch"), axis=1, tiled=True),
+        jnp.concatenate(lax.all_gather(w_branches, ("tm", "batch")), axis=1),
         preferred_element_type=jnp.float32,
     )
     proj = proj.reshape(4, games, block_len, chans)

time: 496 us -> 496 us (level)
  waiting for transfers between devices: 256 us -> 240 us
  local copies, waits for them, and re-layouts: 133 us -> 147 us
    all_gather x1, waiting for transfers between devices: 35.9 us -> 18.8 us  [shards(): lax.all_gather(embedded, 'width', axis=2, tiled=True).reshape(count, -1)]
    all_gather x0 -> x1, local copies, waits for them, and re-layouts: none -> 14 us  [shards(): lax.all_gather(w_branches, ('tm', 'batch'))]
  transfers between devices with their start and end apart: 9 -> 9, of which waited for: 8 -> 8; matrix products, arithmetic and copies ran while one was open for 37% -> 40% of each run, Pallas kernels for 0% -> 0%
where the time goes in v1:
time: 496 us; the launch traced here: 493 us
  waiting for transfers between devices  240 us (48%)
  local copies, waits for them, and re-layouts  147 us (30%)
  other arithmetic  48.4 us (10%)
  matrix products  21.2 us (4%)
  starting transfers between devices  16.6 us (3%)
  between operations  14.6 us (3%)
    all_gather x1, waiting for transfers between devices, shards(): lax.all_gather(w_branches, ('tm', 'batch'))  130 us
    slice x52, local copies, waits for them, and re-layouts, shards(): summed, local = lax.associative_scan(link, (log_a, drive), axis=1)  94.9 us
    reduce_scatter x1, waiting for transfers between devices, shards(): lax.psum_scatter(partial_down, 'width', scatter_dimension=1, tiled=True)  55.3 us
    pad x28, local copies, waits for them, and re-layouts, shards(): summed, local = lax.associative_scan(link, (log_a, drive), axis=1)  29.4 us
    psum x1, waiting for transfers between devices, shards(): lax.psum((local_logits, local_value, local_sq), 'width')  28.3 us
    all_gather x1, waiting for transfers between devices, shards(): lax.all_gather(embedded, 'width', axis=2, tiled=True).reshape(count, -1)  18.8 us
    add x13, other arithmetic, link(): return (early[0] + late[0], jnp.exp(late[0]) * early[1] + late[1])  17.8 us
    ppermute x4, starting transfers between devices, from_behind(): lax.ppermute(value, axis, [(source, source + steps) for source in range(i...  16.4 us
  transfers between devices with their start and end apart: 9, of which 8 were waited for; matrix products, arithmetic and copies ran while one was open for 40% of the time, Pallas kernels for 0%

profile of v1, /device:TPU:0, one launch (start us, length us, event | category | flops | bytes accessed | tf_op | source)
XLA Modules:
  0.0 492.7 jit_solution(13747978678875757608)
XLA Ops:
  9.5 129.8 %all-gather.9.cloned.1.call-done = bf16[64,128,1024]{2,1,0:T(8,128)(2,1)} async-done(((bf16[4,128,1024]{2,1,0:T(8,128)(2,1)}), bf16[64,128,1024]{2,1,0:T(8,128)(2,1)}) %all-gather.9.cloned.1.call-update) | async-done | bytes 16777232 | tf_op jit(solution)/shard_map/all_gather | solution.py:40
  139.4 14.0 %copy.25 = bf16[16,4,128,1024]{3,2,0,1:T(8,128)(2,1)} copy(bf16[16,4,128,1024]{3,2,1,0:T(8,128)(2,1)} %bitcast.50) | data formatting | bytes 33554432 | tf_op jit(solution)/shard_map/all_gather | solution.py:40
  153.4 18.8 %all-gather.5.cloned.1.call-done = bf16[2,256,2048]{2,1,0:T(8,128)(2,1)} async-done(((bf16[2,256,1024]{2,1,0:T(8,128)(2,1)}), bf16[2,256,2048]{2,1,0:T(8,128)(2,1)}) %all-gather.5.cloned.1.call-update) | async-done | bytes 2097168 | tf_op jit(solution)/shard_map/all_gather | solution.py:36
  172.2 12.5 %convolution_bitcast_fusion = f32[4,512,1024]{2,1,0:T(8,128)S(1)} fusion(bf16[512,2048,1]{1,0,2:T(8,128)(2,1)} %bitcast.81, bf16[4,2048,1024]{2,1,0:T(8,128)(2,1)} %bitcast.51), kind=kOutput, calls=%fused_computation.1 | convolution fusion | flops 8589934592 | bytes 27262976 | tf_op jit(solution)/shard_map/td,kdn->ktn/dot_general | solution.py:37
  184.7 2.9 fusion.30
  189.0 3.6 collective-permute-start.1
  194.1 7.6 %fusion.4 = (f32[2,256,1024]{2,1,0:T(8,128)S(1)}, f32[2,256,1024]{2,1,0:T(8,128)}) fusion(f32[2,3,1024]{2,1,0:T(4,128)S(1)} %collective-permute-done.1, f32[2,256,1024]{2,1,0:T(8,128)} %bitcast.53, f32[2,256,1024]{2,1,0:T(8,128)} %bitcast.56, f32[1024]{0:T(1024)S(1)} %bitcast.75, f32[1024]{0:T(1024)S(1)} %bitcast.76, f32[1024]{0:T(1024)S(1)} %bitcast.74, ...), kind=kLoop, calls=%fused_computation.9 | loop fusion | flops 12058624 | bytes 10539008 | tf_op jit(solution)/shard_map/mul | solution.py:55
  207.5 5.4 %slice.297 = f32[2,128,1024]{2,1,0:T(8,128)} slice(f32[2,256,1024]{2,1,0:T(8,128)} %get-tuple-element.48), slice={[0:2:1], [1:256:2], [0:1024:1]} | slice | bytes 2097152 | tf_op jit(solution)/shard_map/slice | solution.py:56
  212.9 5.4 %slice.301 = f32[2,128,1024]{2,1,0:T(8,128)} slice(f32[2,256,1024]{2,1,0:T(8,128)} %get-tuple-element.48), slice={[0:2:1], [0:255:2], [0:1024:1]} | slice | bytes 2097152 | tf_op jit(solution)/shard_map/slice | solution.py:56
  218.3 4.2 multiply_add_fusion.1
  222.5 3.3 slice.304
  225.8 3.3 slice.305
  229.0 3.3 slice.303
  232.3 3.2 slice.307
  290.1 3.3 slice.302
  293.4 3.3 slice.351
  299.6 5.6 %slice.296 = f32[2,127,1024]{2,1,0:T(8,128)} slice(f32[2,256,1024]{2,1,0:T(8,128)} %get-tuple-element.48), slice={[0:2:1], [2:256:2], [0:1024:1]} | slice | bytes 2080768 | tf_op jit(solution)/shard_map/slice | solution.py:56
  305.2 3.0 slice.353
  318.4 5.5 %pad.129 = f32[2,256,1024]{2,1,0:T(8,128)} pad(f32[2,128,1024]{2,1,0:T(8,128)} %add.338, f32[]{:T(128)} %constant.6.clone.1), padding=0_0_0x1_0_1x0_0_0 | pad | bytes 3145732 | tf_op jit(solution)/shard_map/pad | solution.py:56
  325.8 3.0 pad.110
  337.8 5.4 %pad.128 = f32[2,256,1024]{2,1,0:T(8,128)} pad(f32[2,128,1024]{2,1,0:T(8,128)} %pad_maximum_fusion.2, f32[]{:T(128)} %constant.6.clone.1), padding=0_0_0x0_1_1x0_0_0 | pad | bytes 3145732 | tf_op jit(solution)/shard_map/pad | solution.py:56
  344.1 5.5 %pad.113 = f32[2,256,1024]{2,1,0:T(8,128)} pad(f32[2,128,1024]{2,1,0:T(8,128)} %add.322, f32[]{:T(128)} %constant.6.clone.1), padding=0_0_0x1_0_1x0_0_0 | pad | bytes 3145732 | tf_op jit(solution)/shard_map/pad | solution.py:56
  351.9 5.5 %pad.112 = f32[2,256,1024]{2,1,0:T(8,128)} pad(f32[2,128,1024]{2,1,0:T(8,128)} %pad_maximum_fusion.1, f32[]{:T(128)} %constant.6.clone.1), padding=0_0_0x0_1_1x0_0_0 | pad | bytes 3145732 | tf_op jit(solution)/shard_map/pad | solution.py:56
  358.3 18.7 %while.12 = (s32[]{:T(128)}, f32[2,1024]{1,0:T(2,128)S(1)}, f32[2,1024]{1,0:T(2,128)}, f32[2,1024]{1,0:T(2,128)S(1)}, f32[2,1024]{1,0:T(2,128)S(1)}, /*index=5*/s32[]{:T(128)}) while((s32[]{:T(128)}, f32[2,1024]{1,0:T(2,128)S(1)}, f32[2,1024]{1,0:T(2,128)}, f32[2,1024]{1,0:T(2,128)S(1)}, f32[2,1024]{1,0:T(2,128)S(1)}, ...), condition=%wide.region_1.0_spmd, body=%wide.region_0.0_spmd.sunk | while | flops 4098 | bytes 98441 | solution.py:65
  358.4 4.5 collective-permute-start
  364.8 4.2 collective-permute-start
  370.9 4.2 collective-permute-start
  377.0 5.8 %fusion.16 = bf16[2,256,1024]{2,1,0:T(8,128)(2,1)} fusion(f32[2,256,1024]{2,1,0:T(8,128)} %bitcast.54, f32[2,256,1024]{2,1,0:T(8,128)} %pad.128, f32[2,256,1024]{2,1,0:T(8,128)S(1)} %copy-done.4, f32[2,256,1024]{2,1,0:T(8,128)} %pad.112, f32[2,256,1024]{2,1,0:T(8,128)} %pad.113, f32[2,1024]{1,0:T(2,128)} %get-tuple-element.28), kind=kLoop, calls=%fused_computation.21 | loop fusion | flops 7340032 | bytes 11542528 | tf_op jit(solution)/shard_map/convert_element_type | solution.py:69
  382.8 6.9 %fusion.35 = f32[512,2048]{1,0:T(8,128)} fusion(bf16[512,1024]{1,0:T(8,128)(2,1)} %bitcast.57, bf16[2048,1024]{1,0:T(8,128)(2,1)} %all-gather.7.cloned.1.call-done), kind=kOutput, calls=%fused_computation.100 | convolution fusion | flops 2147483648 | bytes 9437184 | tf_op jit(solution)/shard_map/dot_general | solution.py:70
  389.8 55.3 %reduce-scatter.2.cloned.1.call-done = f32[512,1024]{1,0:T(8,128)} async-done(((f32[512,2048]{1,0:T(8,128)}), f32[512,1024]{1,0:T(8,128)}) %reduce-scatter.2.cloned.1.call-update) | async-done | bytes 2097168 | tf_op jit(solution)/shard_map/reduce_scatter | solution.py:76
  449.1 4.9 all-reduce.32
  454.1 28.3 %all-reduce.35.cloned.1.call-done = f32[512,362]{0,1:T(8,128)} async-done(((f32[512,362]{0,1:T(8,128)}), f32[512,362]{0,1:T(8,128)}) %all-reduce.35.cloned.1.call-update) | async-done | bytes 741392 | tf_op jit(solution)/shard_map/psum | solution.py:82
  (234 shorter events, 106.8 us)
Async XLA Ops:
  7.2 439.9 %copy-start = (bf16[1024,362]{0,1:T(8,128)(2,1)S(1)}, bf16[1024,362]{0,1:T(8,128)(2,1)}, u32[]{:S(2)}) copy-start(bf16[1024,362]{0,1:T(8,128)(2,1)} %param.22) | copy-start | bytes 2224132
  7.2 2.3 copy-start.34
  7.2 132.2 %all-gather.9.cloned.1.call-start = ((), (), s32[]{:S(2)}) async-start(), calls=%async_computation.5 | async-start | bytes 17825792 | tf_op jit(solution)/shard_map/all_gather | solution.py:40
  7.9 164.3 %all-gather.5.cloned.1.call-start = ((), (), s32[]{:S(2)}) async-start(), calls=%async_computation.1 | async-start | bytes 3145728 | tf_op jit(solution)/shard_map/all_gather | solution.py:36
  8.7 374.1 %all-gather.7.cloned.1.call-start = ((), (), s32[]{:S(2)}) async-start(), calls=%async_computation.2 | async-start | bytes 4456448 | tf_op jit(solution)/shard_map/all_gather | solution.py:72
  9.4 435.6 %reduce-scatter.2.cloned.1.call-start = ((), (), s32[]{:S(2)}) async-start(), calls=%async_computation.3 | async-start | bytes 6291456 | tf_op jit(solution)/shard_map/reduce_scatter | solution.py:76
  184.7 7.8 %copy-start.35 = (f32[1024]{0:T(1024)S(1)}, f32[1024]{0:T(1024)}, u32[]{:S(2)}) copy-start(f32[1024]{0:T(1024)} %param.20) | copy-start | bytes 12292
  189.0 5.2 %collective-permute-start.1 = (f32[2,3,1024]{2,1,0:T(4,128)S(1)}, f32[2,3,1024]{2,1,0:T(4,128)S(1)}, u32[]{:S(2)}, u32[]{:S(2)}) collective-permute-start(f32[2,3,1024]{2,1,0:T(4,128)S(1)} %slice.375), channel_id=1, source_target_pairs={{0,8},{8,16},{16,24},{1,9},{9,17},{17,25},{2,10},{10,18},{18,26},{... | collective-permute-start | bytes 73736 | tf_op jit(solution)/shard_map/ppermute | solution.py:13
  299.6 10.6 %copy-start.18 = (f32[2,2,1024]{2,1,0:T(2,128)S(1)}, f32[2,2,1024]{2,1,0:T(2,128)}, u32[]{:S(2)}) copy-start(f32[2,2,1024]{2,1,0:T(2,128)} %slice.335) | copy-start | bytes 49156
  299.6 10.6 %copy-start.19 = (f32[2,2,1024]{2,1,0:T(2,128)S(1)}, f32[2,2,1024]{2,1,0:T(2,128)}, u32[]{:S(2)}) copy-start(f32[2,2,1024]{2,1,0:T(2,128)} %slice.333) | copy-start | bytes 49156
  299.6 10.6 %copy-start.20 = (f32[2,2,1024]{2,1,0:T(2,128)S(1)}, f32[2,2,1024]{2,1,0:T(2,128)}, u32[]{:S(2)}) copy-start(f32[2,2,1024]{2,1,0:T(2,128)} %slice.337) | copy-start | bytes 49156
  299.6 10.8 %copy-start.15 = (f32[1,8,1024]{2,1,0:T(8,128)S(1)}, f32[1,8,1024]{2,1,0:T(8,128)}, u32[]{:S(2)}) copy-start(f32[1,8,1024]{2,1,0:T(8,128)} %get-tuple-element.103) | copy-start | bytes 98308
  299.6 11.1 %copy-start.16 = (f32[2,3,1024]{2,1,0:T(4,128)S(1)}, f32[2,3,1024]{2,1,0:T(4,128)}, u32[]{:S(2)}) copy-start(f32[2,3,1024]{2,1,0:T(4,128)} %slice.326) | copy-start | bytes 73732
  299.6 11.1 %copy-start.17 = (f32[2,3,1024]{2,1,0:T(4,128)S(1)}, f32[2,3,1024]{2,1,0:T(4,128)}, u32[]{:S(2)}) copy-start(f32[2,3,1024]{2,1,0:T(4,128)} %slice.343) | copy-start | bytes 73732
  305.2 5.6 %copy-start.32 = (f32[2,1,1024]{2,1,0:T(1,128)S(1)}, f32[2,1,1024]{2,1,0:T(1,128)}, u32[]{:S(2)}) copy-start(f32[2,1,1024]{2,1,0:T(1,128)} %slice.411) | copy-start | bytes 24580
  305.2 5.7 %copy-start.31 = (f32[2,1,1024]{2,1,0:T(1,128)S(1)}, f32[2,1,1024]{2,1,0:T(1,128)}, u32[]{:S(2)}) copy-start(f32[2,1,1024]{2,1,0:T(1,128)} %slice.385) | copy-start | bytes 24580
  305.2 5.8 %copy-start.13 = (f32[2,7,1024]{2,1,0:T(8,128)S(1)}, f32[2,7,1024]{2,1,0:T(8,128)}, u32[]{:S(2)}) copy-start(f32[2,7,1024]{2,1,0:T(8,128)} %slice.320) | copy-start | bytes 172036
  305.2 5.8 %copy-start.14 = (f32[2,7,1024]{2,1,0:T(8,128)S(1)}, f32[2,7,1024]{2,1,0:T(8,128)}, u32[]{:S(2)}) copy-start(f32[2,7,1024]{2,1,0:T(8,128)} %slice.345) | copy-start | bytes 172036
  305.2 5.9 %copy-start.30 = (f32[2,1,1024]{2,1,0:T(1,128)S(1)}, f32[2,1,1024]{2,1,0:T(1,128)}, u32[]{:S(2)}) copy-start(f32[2,1,1024]{2,1,0:T(1,128)} %slice.410) | copy-start | bytes 24580
  308.2 3.1 copy-start.29
  318.4 5.5 %copy-start.23 = (f32[2,1,1024]{2,1,0:T(1,128)S(1)}, f32[2,1,1024]{2,1,0:T(1,128)}, u32[]{:S(2)}) copy-start(f32[2,1,1024]{2,1,0:T(1,128)} %slice.381) | copy-start | bytes 24580
  330.8 2.9 copy-start.1
  330.8 2.9 copy-start.2
  330.8 2.9 copy-start.6
  333.7 2.9 copy-start.22
  337.8 5.4 %copy-start.4 = (f32[2,256,1024]{2,1,0:T(8,128)S(1)}, f32[2,256,1024]{2,1,0:T(8,128)}, u32[]{:S(2)}) copy-start(f32[2,256,1024]{2,1,0:T(8,128)} %pad.129) | copy-start | bytes 6291460
  343.2 6.4 %copy-start.21 = (f32[2,1,1024]{2,1,0:T(1,128)S(1)}, f32[2,1,1024]{2,1,0:T(1,128)}, u32[]{:S(2)}) copy-start(f32[2,1,1024]{2,1,0:T(1,128)} %slice.380) | copy-start | bytes 24580
  358.4 5.8 %collective-permute-start = (f32[2,1024]{1,0:T(2,128)S(1)}, f32[2,1024]{1,0:T(2,128)S(1)}, u32[]{:S(2)}, u32[]{:S(2)}) collective-permute-start(f32[2,1024]{1,0:T(2,128)S(1)} %get-tuple-element.135), channel_id=1, source_target_pairs={{0,8},{8,16},{16,24},{1,9},{9,17},{17,25},{2,10},{10,18},{18,26},{... | collective-permute-start | bytes 24584 | tf_op jit(solution)/shard_map/while/body/eval_jaxpr/ppermute | solution.py:13
  364.8 5.5 %collective-permute-start = (f32[2,1024]{1,0:T(2,128)S(1)}, f32[2,1024]{1,0:T(2,128)S(1)}, u32[]{:S(2)}, u32[]{:S(2)}) collective-permute-start(f32[2,1024]{1,0:T(2,128)S(1)} %get-tuple-element.135), channel_id=1, source_target_pairs={{0,8},{8,16},{16,24},{1,9},{9,17},{17,25},{2,10},{10,18},{18,26},{... | collective-permute-start | bytes 24584 | tf_op jit(solution)/shard_map/while/body/eval_jaxpr/ppermute | solution.py:13
  370.9 5.5 %collective-permute-start = (f32[2,1024]{1,0:T(2,128)S(1)}, f32[2,1024]{1,0:T(2,128)S(1)}, u32[]{:S(2)}, u32[]{:S(2)}) collective-permute-start(f32[2,1024]{1,0:T(2,128)S(1)} %get-tuple-element.135), channel_id=1, source_target_pairs={{0,8},{8,16},{16,24},{1,9},{9,17},{17,25},{2,10},{10,18},{18,26},{... | collective-permute-start | bytes 24584 | tf_op jit(solution)/shard_map/while/body/eval_jaxpr/ppermute | solution.py:13
  389.7 55.3 %copy-start.5 = (bf16[2,256,1024]{2,1,0:T(8,128)(2,1)S(1)}, bf16[2,256,1024]{2,1,0:T(8,128)(2,1)}, u32[]{:S(2)}) copy-start(bf16[2,256,1024]{2,1,0:T(8,128)(2,1)} %param.16) | copy-start | bytes 3145732
  389.7 92.6 %all-reduce.35.cloned.1.call-start = ((), (), s32[]{:S(2)}) async-start(), calls=%async_computation.4 | async-start | bytes 1507328 | tf_op jit(solution)/shard_map/psum | solution.py:82
  (19 other events, 21.4 us)
Sparse Core Ops, SparseCore 0:
  10.2 129.1 all-gather.8
  140.9 31.2 all-gather.4
  174.4 50.3 all-gather.6
  389.8 55.1 reduce-scatter.1
  448.7 33.6 all-reduce.34
